TPU v7x, 32 devices: a whole 2x2x4 slice. The times are simulated.
32 devices in a mesh: dp: 8 (over y, x, core), tensor: 4 (over z).
Axes of the slice: x: 2, y: 2, z: 4, core: 2. Of those that a mesh axis runs over, the one named last changes fastest.
Arguments:
- acts: bfloat16 [8192, 3584], P('dp'), may hold values from -6 to 6
- cotangent: bfloat16 [8192, 18944], P('dp', 'tensor'), may hold values from -6 to 6
- hessian_ema: float32 [3584, 18944], P('dp', 'tensor'), may hold values from 0.02 to 2
- momentum: float32 [3584, 18944], P('dp', 'tensor'), may hold values from -0.12 to 0.12
- gamma_table: float32 [28], replicated, may hold values from 0.005 to 0.02
- layer_index: int32 [1], replicated, may hold values from 0 to 27
- step_count: int32 [1], replicated, may hold values from 1 to 20
Outputs:
- new_hessian: float32 [67895296], P(('dp', 'tensor'))
- ratio: float32 [67895296], P(('dp', 'tensor'))
All inputs are finite; a program needn't handle non-finite values.
Results may differ from a plain program's by a relative error of at most 0.0003.
Values sent between devices are 32-bit elements; how exact they have to be, the bound alone decides.
A program may use at most 192 MiB of HBM per device.

v0:
```python
import jax
import jax.numpy as jnp
from jax import lax
from jax.sharding import PartitionSpec as P


def settle(grad_part, hess_part, mom_part, tokens_all, gamma, correction):
    estimate = grad_part * grad_part / tokens_all
    fresh = 0.99 * hess_part + 0.01 * estimate
    corrected = fresh / correction
    ratio = jnp.clip(mom_part / (gamma * corrected), -1.0, 1.0)
    return (fresh, ratio)


def on_device(acts, cotangent, hessian_ema, momentum, gamma_table, layer_index, step_count):
    tokens_all = float(acts.shape[0] * lax.axis_size("dp"))
    picks = jnp.arange(gamma_table.shape[0], dtype=jnp.int32) == layer_index[0]
    gamma = jnp.sum(jnp.where(picks, gamma_table, jnp.zeros_like(gamma_table)))
    correction = 1.0 - jnp.power(
        jnp.asarray(0.99, gamma_table.dtype), step_count[0].astype(gamma_table.dtype)
    )
    grad_rows = lax.psum_scatter(
        lax.dot_general(
            acts, cotangent, (((0,), (0,)), ((), ())), preferred_element_type=jnp.float32
        ),
        "dp",
        scatter_dimension=0,
        tiled=True,
    )
    moved_grad, moved_hess, moved_mom = (
        lax.all_to_all(grad_rows, "tensor", split_axis=0, concat_axis=1, tiled=True),
        lax.all_to_all(hessian_ema, "tensor", split_axis=0, concat_axis=1, tiled=True),
        lax.all_to_all(momentum, "tensor", split_axis=0, concat_axis=1, tiled=True),
    )
    fresh, ratio = settle(moved_grad, moved_hess, moved_mom, tokens_all, gamma, correction)
    return (fresh.reshape(-1), ratio.reshape(-1))


def solution(mesh):
    placed = (P("dp", None), P("dp", "tensor"), P("dp", "tensor"), P("dp", "tensor"), P(), P(), P())
    return jax.shard_map(
        on_device,
        mesh=mesh,
        in_specs=placed,
        out_specs=(P(("dp", "tensor")), P(("dp", "tensor"))),
        check_vma=False,
    )
```

profile of v0, /device:TPU:0, one launch (start us, length us, event | category | flops | bytes accessed | tf_op | source)
XLA Modules:
  0.0 698.3 jit_solution(11572785254212841880)
XLA Ops:
  7.2 0.0 reduce-scatter.2.cloned.1.call-start
  7.2 45.5 %fusion.1 = f32[3584,4736]{1,0:T(8,128)} fusion(bf16[1024,3584]{1,0:T(8,128)(2,1)} %param.7, bf16[1024,4736]{1,0:T(8,128)(2,1)} %param.8), kind=kOutput, calls=%fused_computation.4 | convolution fusion | flops 34762391552 | bytes 84934656 | tf_op jit(solution)/shard_map/dot_general | solution.py:23
  52.7 0.0 reduce-scatter.2.cloned.1.call-update
  52.7 0.0 copy-start
  52.7 195.0 %all_to_all.45 = f32[4,112,4736]{2,1,0:T(8,128)} all-to-all(f32[4,112,4736]{2,1,0:T(8,128)} %bitcast.12), channel_id=1, replica_groups=mesh['dp'=8,'tensor'=4] {'tensor'}, dimensions={0} | all-to-all | bytes 16973824 | tf_op jit(solution)/shard_map/all_to_all | solution.py:32
  247.7 0.0 copy-done
  247.7 188.6 %all_to_all.46 = f32[4,112,4736]{2,1,0:T(8,128)} all-to-all(f32[4,112,4736]{2,1,0:T(8,128)S(1)} %bitcast.13), channel_id=1, replica_groups=mesh['dp'=8,'tensor'=4] {'tensor'}, dimensions={0} | all-to-all | bytes 16973824 | tf_op jit(solution)/shard_map/all_to_all | solution.py:33
  436.3 22.5 %reduce-scatter.2.cloned.1.call-done = f32[448,4736]{1,0:T(8,128)} async-done(((f32[3584,4736]{1,0:T(8,128)}), f32[448,4736]{1,0:T(8,128)}) %reduce-scatter.2.cloned.1.call-update) | async-done | bytes 8486928 | tf_op jit(solution)/shard_map/reduce_scatter | solution.py:22
  458.9 0.0 copy-start.1
  458.9 6.0 all-to-all-start.1
  466.2 0.0 copy-done.1
  466.2 0.6 fusion
  466.8 10.1 %copy.13 = f32[112,4,4736]{2,1,0:T(4,128)} copy(f32[112,4,4736]{2,0,1:T(8,128)} %bitcast.11) | data formatting | bytes 16973824 | tf_op jit(solution)/shard_map/all_to_all | solution.py:33
  476.9 10.4 %all_to_all.41 = f32[2121728]{0:T(1024)} reshape(f32[112,4,4736]{2,1,0:T(4,128)} %copy.13) | data formatting | bytes 16973824 | tf_op jit(solution)/shard_map/all_to_all | solution.py:33
  487.3 162.7 %all-to-all-done.1 = f32[4,112,4736]{2,1,0:T(8,128)} async-done(((f32[4,112,4736]{2,1,0:T(8,128)}), f32[4,112,4736]{2,1,0:T(8,128)}, u32[]{:S(2)}, u32[]{:S(2)}) %all-to-all-start.1) | async-done | bytes 8486944 | tf_op jit(solution)/shard_map/all_to_all | solution.py:31
  650.0 10.5 %add_bitcast_fusion = f32[112,4,4736]{2,0,1:T(8,128)} fusion(f32[4,112,4736]{2,1,0:T(8,128)} %all-to-all-done.1, f32[4,112,4736]{2,1,0:T(8,128)} %all_to_all.45), kind=kLoop, calls=%fused_computation.1 | loop fusion | flops 8486912 | bytes 25460736 | tf_op jit(solution)/shard_map/add | solution.py:9
  660.5 9.9 %copy.12 = f32[112,4,4736]{2,1,0:T(4,128)} copy(f32[112,4,4736]{2,0,1:T(8,128)} %add_bitcast_fusion) | data formatting | bytes 16973824 | tf_op jit(solution)/shard_map/add | solution.py:9
  670.5 10.3 %add.15 = f32[2121728]{0:T(1024)} reshape(f32[112,4,4736]{2,1,0:T(4,128)} %copy.12) | data formatting | bytes 16973824 | tf_op jit(solution)/shard_map/add | solution.py:9
  680.8 10.7 %divide_clamp_fusion = f32[2121728]{0:T(1024)} fusion(f32[2121728]{0:T(1024)} %all_to_all.41, f32[2121728]{0:T(1024)} %add.15, f32[]{:T(128)} %bitcast.6, f32[]{:T(128)} %fusion), kind=kLoop, calls=%fused_computation | loop fusion | flops 8486912 | bytes 25460744 | tf_op jit(solution)/shard_map/jit(clip)/min | solution.py:11
Async XLA Ops:
  7.2 451.7 %reduce-scatter.2.cloned.1.call-start = ((), (), s32[]{:S(2)}) async-start(), calls=%async_computation.4 | async-start | bytes 76382208 | tf_op jit(solution)/shard_map/reduce_scatter | solution.py:22
  52.7 195.0 %copy-start = (f32[448,4736]{1,0:T(8,128)S(1)}, f32[448,4736]{1,0:T(8,128)}, u32[]{:S(2)}) copy-start(f32[448,4736]{1,0:T(8,128)} %param.10) | copy-start | bytes 25460740
  458.9 7.3 %copy-start.1 = (f32[28]{0:T(128)S(1)}, f32[28]{0:T(128)}, u32[]{:S(2)}) copy-start(f32[28]{0:T(128)} %param.11) | copy-start | bytes 340
  458.9 191.1 %all-to-all-start.1 = ((f32[4,112,4736]{2,1,0:T(8,128)}), f32[4,112,4736]{2,1,0:T(8,128)}, u32[]{:S(2)}, u32[]{:S(2)}) async-start(f32[4,112,4736]{2,1,0:T(8,128)} %bitcast.14), calls=%async_computation.2 | async-start | bytes 16973824 | tf_op jit(solution)/shard_map/all_to_all | solution.py:31
Sparse Core Ops, SparseCore 0:
  52.8 405.9 reduce-scatter.1
where the time goes:
time: 699 us; the launch traced here: 698 us
  blocking collectives  384 us (55%)
  waiting for transfers between devices  185 us (26%)
  matrix products  45.5 us (7%)
  local copies, waits for them, and re-layouts  40.8 us (6%)
  other arithmetic  21.8 us (3%)
  between operations  15.4 us (2%)
    all_to_all x1, blocking collectives, on_device(): lax.all_to_all(hessian_ema, 'tensor', split_axis=0, concat_axis=1, tiled=...  195 us
    all_to_all x1, blocking collectives, on_device(): lax.all_to_all(momentum, 'tensor', split_axis=0, concat_axis=1, tiled=True)  189 us
    all_to_all x1, waiting for transfers between devices, on_device(): lax.all_to_all(grad_rows, 'tensor', split_axis=0, concat_axis=1, tiled=True)  163 us
    dot_general x1, matrix products, on_device(): lax.dot_general(acts, cotangent, (((0,), (0,)), ((), ())), preferred_elem...  45.5 us
    reduce_scatter x1, waiting for transfers between devices, on_device(): lax.psum_scatter(lax.dot_general(acts, cotangent, (((0,), (0,)), ((), ())...  22.5 us
    all_to_all x2, local copies, waits for them, and re-layouts, on_device(): lax.all_to_all(momentum, 'tensor', split_axis=0, concat_axis=1, tiled=True)  20.5 us
    add x2, local copies, waits for them, and re-layouts, settle(): fresh = 0.99 * hess_part + 0.01 * estimate  20.3 us
  transfers between devices with their start and end apart: 2, of which 2 were waited for; matrix products, arithmetic and copies ran while one was open for 2% of the time, Pallas kernels for 0%

commit v1 on v0

v1 whole, which is shorter than its diff:
```python
import jax
import jax.numpy as jnp
from jax import lax
from jax.sharding import PartitionSpec as P

SHARES = (2, 2, 2, 1)
EARLY = 2


def settle(grad_part, hess_part, mom_part, tokens_all, gamma, correction):
    estimate = grad_part * grad_part / tokens_all
    fresh = 0.99 * hess_part + 0.01 * estimate
    corrected = fresh / correction
    ratio = jnp.clip(mom_part / (gamma * corrected), -1.0, 1.0)
    return (fresh, ratio)


def swap(block):
    return lax.all_to_all(block, "tensor", split_axis=0, concat_axis=1, tiled=True)


def cuts_of(rows):
    unit = next(u for u in (16, 8, 4, 2, 1) if rows % u == 0)
    units, total, edges, upto = rows // unit, sum(SHARES), [0], 0
    for share in SHARES:
        upto += share
        edges.append(unit * (units * upto // total))
    return list(zip(edges, edges[1:]))


def on_device(acts, cotangent, hessian_ema, momentum, gamma_table, layer_index, step_count):
    dp = lax.axis_size("dp")
    tensor = lax.axis_size("tensor")
    tokens_all = float(acts.shape[0] * dp)
    picks = jnp.arange(gamma_table.shape[0], dtype=jnp.int32) == layer_index[0]
    gamma = jnp.sum(jnp.where(picks, gamma_table, jnp.zeros_like(gamma_table)))
    correction = 1.0 - jnp.power(
        jnp.asarray(0.99, gamma_table.dtype), step_count[0].astype(gamma_table.dtype)
    )
    width = cotangent.shape[1]
    rows = hessian_ema.shape[0] // tensor
    whole = tensor * width
    acts_rows = acts.T.reshape(dp * tensor, rows, acts.shape[0])
    hess_rows = hessian_ema.reshape(tensor, rows, width)
    mom_rows = momentum.reshape(tensor, rows, width)
    cuts = cuts_of(rows)

    def block(states, a, b):
        return states[:, a:b].reshape(tensor * (b - a), width)

    partials = []
    for a, b in cuts:
        partial = lax.dot_general(
            acts_rows[:, a:b].reshape(dp * tensor * (b - a), acts.shape[0]),
            cotangent,
            (((1,), (0,)), ((), ())),
            preferred_element_type=jnp.float32,
        )
        partial, acts_rows = lax.optimization_barrier((partial, acts_rows))
        partials.append(partial)
    sums = [lax.psum_scatter(p, "dp", scatter_dimension=0, tiled=True) for p in partials]
    late = cuts[EARLY][0]
    moved_hess = swap(block(hess_rows, late, rows))
    moved_mom = swap(block(mom_rows, late, rows))
    sums[0], moved_hess, moved_mom = lax.optimization_barrier(
        (sums[0], moved_hess, moved_mom) + tuple(p[:8, :128] for p in partials[1:])
    )[:3]

    fresh_all = jnp.zeros((rows * whole,), jnp.float32)
    ratio_all = jnp.zeros((rows * whole,), jnp.float32)
    for step, (a, b) in enumerate(cuts):
        if step < EARLY:
            fresh, ratio = settle(
                sums[step], block(hess_rows, a, b), block(mom_rows, a, b), tokens_all, gamma, correction
            )
            fresh, ratio = swap(fresh), swap(ratio)
            if step + 1 < len(cuts):
                sums[step + 1], fresh, ratio = lax.optimization_barrier((sums[step + 1], fresh, ratio))
        else:
            fresh, ratio = settle(
                swap(sums[step]),
                moved_hess[a - late : b - late],
                moved_mom[a - late : b - late],
                tokens_all,
                gamma,
                correction,
            )
        fresh_all = lax.dynamic_update_slice(fresh_all, fresh.reshape(-1), (a * whole,))
        ratio_all = lax.dynamic_update_slice(ratio_all, ratio.reshape(-1), (a * whole,))
    return (fresh_all, ratio_all)


def solution(mesh):
    placed = (P("dp", None), P("dp", "tensor"), P("dp", "tensor"), P("dp", "tensor"), P(), P(), P())
    return jax.shard_map(
        on_device,
        mesh=mesh,
        in_specs=placed,
        out_specs=(P(("dp", "tensor")), P(("dp", "tensor"))),
        check_vma=False,
    )
```

time: 699 us -> 639 us (0.914)
  blocking collectives: 384 us -> 58 us
  waiting for transfers between devices: 185 us -> 343 us
  local copies, waits for them, and re-layouts: 40.8 us -> 93.5 us
  starting transfers between devices: 6.03 us -> 32.7 us
  matrix products: 45.5 us -> 66.7 us
  other arithmetic: 21.8 us -> 28.8 us
    all_to_all x2 -> x1, blocking collectives: 384 us -> 58 us  [swap(): lax.all_to_all(block, 'tensor', split_axis=0, concat_axis=1, tiled=True)]
    all_to_all x1 -> x7, waiting for transfers between devices: 163 us -> 341 us  [swap(): lax.all_to_all(block, 'tensor', split_axis=0, concat_axis=1, tiled=True)]
    all_to_all x1 -> x7, starting transfers between devices: 5.99 us -> 32.4 us  [swap(): lax.all_to_all(block, 'tensor', split_axis=0, concat_axis=1, tiled=True)]
    reduce_scatter x1 -> x4, waiting for transfers between devices: 22.5 us -> 0.03 us  [on_device(): lax.psum_scatter(p, 'dp', scatter_dimension=0, tiled=True)]
    dot_general x1 -> x4, matrix products: 45.5 us -> 66.7 us  [on_device(): lax.dot_general(acts_rows[:, a:b].reshape(dp * tensor * (b - a), acts.sha...]
    slice x0 -> x7, local copies, waits for them, and re-layouts: none -> 20.6 us  [the longest x3 13.5 us: block(): return states[:, a:b].reshape(tensor * (b - a), width)]
    add x2 -> x0, local copies, waits for them, and re-layouts: 20.3 us -> none  [settle(): fresh = 0.99 * hess_part + 0.01 * estimate]
    dynamic_update_slice x0 -> x7, local copies, waits for them, and re-layouts: none -> 20 us  [the longest x3 10.6 us: on_device(): lax.dynamic_update_slice(fresh_all, fresh.reshape(-1), (a * whole,))]
  transfers between devices with their start and end apart: 2 -> 11, of which waited for: 2 -> 7; matrix products, arithmetic and copies ran while one was open for 2% -> 22% of each run, Pallas kernels for 0% -> 0%
where the time goes in v1:
time: 639 us; the launch traced here: 637 us
  waiting for transfers between devices  343 us (54%)
  local copies, waits for them, and re-layouts  93.5 us (15%)
  matrix products  66.7 us (10%)
  blocking collectives  58 us (9%)
  starting transfers between devices  32.7 us (5%)
  other arithmetic  28.8 us (5%)
  between operations  15.3 us (2%)
    all_to_all x7, waiting for transfers between devices, swap(): lax.all_to_all(block, 'tensor', split_axis=0, concat_axis=1, tiled=True)  341 us
    dot_general x4, matrix products, on_device(): lax.dot_general(acts_rows[:, a:b].reshape(dp * tensor * (b - a), acts.sha...  66.7 us
    all_to_all x1, blocking collectives, swap(): lax.all_to_all(block, 'tensor', split_axis=0, concat_axis=1, tiled=True)  58 us
    all_to_all x7, starting transfers between devices, swap(): lax.all_to_all(block, 'tensor', split_axis=0, concat_axis=1, tiled=True)  32.4 us
    min x4, other arithmetic, settle(): ratio = jnp.clip(mom_part / (gamma * corrected), -1.0, 1.0)  22.2 us
    all_to_all x6, local copies, waits for them, and re-layouts, swap(): lax.all_to_all(block, 'tensor', split_axis=0, concat_axis=1, tiled=True)  18.5 us
    unnamed x19, local copies, waits for them, and re-layouts  15.9 us
    slice x3, local copies, waits for them, and re-layouts, block(): return states[:, a:b].reshape(tensor * (b - a), width)  13.5 us
  transfers between devices with their start and end apart: 11, of which 7 were waited for; matrix products, arithmetic and copies ran while one was open for 22% of the time, Pallas kernels for 0%

profile of v1, /device:TPU:0, one launch (start us, length us, event | category | flops | bytes accessed | tf_op | source)
XLA Modules:
  0.0 637.5 jit_solution(4189003684720216807)
XLA Ops:
  7.2 10.4 %copy.18 = bf16[1024,3584]{0,1:T(8,128)(2,1)} copy(bf16[1024,3584]{1,0:T(8,128)(2,1)} %param.7) | data formatting | bytes 14680064 | tf_op args[0]
  19.4 17.3 %fusion.4 = f32[1024,4736]{1,0:T(8,128)} fusion(bf16[1024,1024]{1,0:T(8,128)(2,1)S(1)} %bitcast.91, bf16[1024,4736]{1,0:T(8,128)(2,1)} %param.8), kind=kOutput, calls=%fused_computation.23 | convolution fusion | flops 9932111872 | bytes 31195136 | tf_op jit(solution)/shard_map/dot_general | solution.py:53
  38.7 18.3 %fusion.5 = f32[1024,4736]{1,0:T(8,128)} fusion(bf16[1024,1024]{1,0:T(8,128)(2,1)S(1)} %bitcast.92, bf16[1024,4736]{1,0:T(8,128)(2,1)} %param.8), kind=kOutput, calls=%fused_computation.24 | convolution fusion | flops 9932111872 | bytes 31195136 | tf_op jit(solution)/shard_map/dot_general | solution.py:53
  59.3 19.6 %fusion.6 = f32[1024,4736]{1,0:T(8,128)} fusion(bf16[1024,1024]{1,0:T(8,128)(2,1)S(1)} %bitcast.93, bf16[1024,4736]{1,0:T(8,128)(2,1)} %param.8), kind=kOutput, calls=%fused_computation.25 | convolution fusion | flops 9932111872 | bytes 31195136 | tf_op jit(solution)/shard_map/dot_general | solution.py:53
  80.2 11.5 %fusion.7 = f32[512,4736]{1,0:T(8,128)} fusion(bf16[512,1024]{1,0:T(8,128)(2,1)S(1)} %bitcast.95, bf16[1024,4736]{1,0:T(8,128)(2,1)} %param.8), kind=kOutput, calls=%fused_computation.26 | convolution fusion | flops 4966055936 | bytes 20447232 | tf_op jit(solution)/shard_map/dot_general | solution.py:53
  96.6 6.6 %all-to-all-start = ((f32[4,48,4736]{2,1,0:T(8,128)}), f32[4,48,4736]{2,1,0:T(8,128)}, u32[]{:S(2)}, u32[]{:S(2)}) async-start(f32[4,48,4736]{2,1,0:T(8,128)} %slice.61), calls=%async_computation.2 | async-start | bytes 7274496 | tf_op jit(solution)/shard_map/all_to_all | solution.py:19
  108.1 76.6 %all-to-all-done = f32[4,48,4736]{2,1,0:T(8,128)} async-done(((f32[4,48,4736]{2,1,0:T(8,128)}), f32[4,48,4736]{2,1,0:T(8,128)}, u32[]{:S(2)}, u32[]{:S(2)}) %all-to-all-start) | async-done | bytes 3637280 | tf_op jit(solution)/shard_map/all_to_all | solution.py:19
  184.7 4.9 all-to-all-start.1
  196.0 5.0 fusion.3
  205.1 65.3 %all-to-all-done.1 = f32[4,48,4736]{2,1,0:T(8,128)} async-done(((f32[4,48,4736]{2,1,0:T(8,128)}), f32[4,48,4736]{2,1,0:T(8,128)}, u32[]{:S(2)}, u32[]{:S(2)}) %all-to-all-start.1) | async-done | bytes 3637280 | tf_op jit(solution)/shard_map/all_to_all | solution.py:19
  270.4 5.1 copy.28
  275.5 6.2 fusion.1
  281.7 58.0 %all_to_all.134 = f32[4,32,4736]{2,1,0:T(8,128)} all-to-all(f32[4,32,4736]{2,1,0:T(8,128)S(1)} %bitcast.84), channel_id=1, replica_groups=mesh['dp'=8,'tensor'=4] {'tensor'}, dimensions={0} | all-to-all | bytes 4849664 | tf_op jit(solution)/shard_map/all_to_all | solution.py:19
  343.3 54.5 %all-to-all-done.3 = f32[4,32,4736]{2,1,0:T(8,128)S(1)} async-done(((f32[4,32,4736]{2,1,0:T(8,128)}), f32[4,32,4736]{2,1,0:T(8,128)S(1)}, u32[]{:S(2)}, u32[]{:S(2)}) %all-to-all-start.3) | async-done | bytes 2424864 | tf_op jit(solution)/shard_map/all_to_all | solution.py:19
  397.8 4.6 all-to-all-start.7
  407.4 8.1 %fusion = (f32[128,4736]{1,0:T(8,128)}, f32[128,4736]{1,0:T(8,128)}) fusion(f32[4,32,4736]{2,1,0:T(8,128)} %get-tuple-element.44, f32[]{:T(128)} %bitcast.13, f32[]{:T(128)} %fusion.2, f32[128,4736]{1,0:T(8,128)} %reduce-scatter.5.cloned.1.call-done, f32[4,32,4736]{2,1,0:T(8,128)} %get-tuple-element.42), kind=kLoop, calls=%fused_computation.3 | loop fusion | flops 4243456 | bytes 12124168 | tf_op jit(solution)/shard_map/jit(clip)/min | solution.py:14
  415.5 15.5 %all-to-all-done.7 = f32[4,16,4736]{2,1,0:T(8,128)} async-done(((f32[4,16,4736]{2,1,0:T(8,128)}), f32[4,16,4736]{2,1,0:T(8,128)}, u32[]{:S(2)}, u32[]{:S(2)}) %all-to-all-start.7) | async-done | bytes 1212448 | tf_op jit(solution)/shard_map/all_to_all | solution.py:19
  431.0 4.5 all-to-all-start.4
  438.1 52.3 %all-to-all-done.4 = f32[4,32,4736]{2,1,0:T(8,128)} async-done(((f32[4,32,4736]{2,1,0:T(8,128)}), f32[4,32,4736]{2,1,0:T(8,128)}, u32[]{:S(2)}, u32[]{:S(2)}) %all-to-all-start.4) | async-done | bytes 2424864 | tf_op jit(solution)/shard_map/all_to_all | solution.py:19
  490.4 4.6 all-to-all-start.5
  507.7 5.6 dynamic_update_slice.24
  513.2 4.7 dynamic_update_slice.28
  519.8 30.1 %all-to-all-done.5 = f32[4,32,4736]{2,1,0:T(8,128)} async-done(((f32[4,32,4736]{2,1,0:T(8,128)}), f32[4,32,4736]{2,1,0:T(8,128)}, u32[]{:S(2)}, u32[]{:S(2)}) %all-to-all-start.5) | async-done | bytes 2424864 | tf_op jit(solution)/shard_map/all_to_all | solution.py:19
  566.2 47.0 %all-to-all-done.6 = f32[4,32,4736]{2,1,0:T(8,128)S(1)} async-done(((f32[4,32,4736]{2,1,0:T(8,128)}), f32[4,32,4736]{2,1,0:T(8,128)S(1)}, u32[]{:S(2)}, u32[]{:S(2)}) %all-to-all-start.6) | async-done | bytes 2424864 | tf_op jit(solution)/shard_map/all_to_all | solution.py:19
  (64 shorter events, 86.1 us)
Async XLA Ops:
  7.2 268.3 %reduce-scatter.7.cloned.1.call-start = ((), (), s32[]{:S(2)}) async-start(), calls=%async_computation.13 | async-start | bytes 21823488 | tf_op jit(solution)/shard_map/reduce_scatter | solution.py:61
  36.7 306.6 %reduce-scatter.11.cloned.1.call-start = ((), (), s32[]{:S(2)}) async-start(), calls=%async_computation.15 | async-start | bytes 10911744 | tf_op jit(solution)/shard_map/reduce_scatter | solution.py:61
  91.7 315.7 %reduce-scatter.5.cloned.1.call-start = ((), (), s32[]{:S(2)}) async-start(), calls=%async_computation.12 | async-start | bytes 21823488 | tf_op jit(solution)/shard_map/reduce_scatter | solution.py:61
  96.6 88.1 %all-to-all-start = ((f32[4,48,4736]{2,1,0:T(8,128)}), f32[4,48,4736]{2,1,0:T(8,128)}, u32[]{:S(2)}, u32[]{:S(2)}) async-start(f32[4,48,4736]{2,1,0:T(8,128)} %slice.61), calls=%async_computation.2 | async-start | bytes 7274496 | tf_op jit(solution)/shard_map/all_to_all | solution.py:19
  103.1 450.0 %reduce-scatter.9.cloned.1.call-start = ((), (), s32[]{:S(2)}) async-start(), calls=%async_computation.14 | async-start | bytes 21823488 | tf_op jit(solution)/shard_map/reduce_scatter | solution.py:61
  108.1 82.9 %copy-start.8 = (f32[28]{0:T(128)S(1)}, f32[28]{0:T(128)}, u32[]{:S(2)}) copy-start(f32[28]{0:T(128)} %param.11) | copy-start | bytes 340
  184.7 85.7 %all-to-all-start.1 = ((f32[4,48,4736]{2,1,0:T(8,128)}), f32[4,48,4736]{2,1,0:T(8,128)}, u32[]{:S(2)}, u32[]{:S(2)}) async-start(f32[4,48,4736]{2,1,0:T(8,128)} %slice.62), calls=%async_computation.3 | async-start | bytes 7274496 | tf_op jit(solution)/shard_map/all_to_all | solution.py:19
  339.7 58.1 %all-to-all-start.3 = ((f32[4,32,4736]{2,1,0:T(8,128)}), f32[4,32,4736]{2,1,0:T(8,128)S(1)}, u32[]{:S(2)}, u32[]{:S(2)}) async-start(f32[4,32,4736]{2,1,0:T(8,128)} %bitcast.82), calls=%async_computation.5 | async-start | bytes 4849664 | tf_op jit(solution)/shard_map/all_to_all | solution.py:19
  397.8 4.6 copy-start.2
  397.8 33.2 %all-to-all-start.7 = ((f32[4,16,4736]{2,1,0:T(8,128)}), f32[4,16,4736]{2,1,0:T(8,128)}, u32[]{:S(2)}, u32[]{:S(2)}) async-start(f32[4,16,4736]{2,1,0:T(8,128)} %bitcast.94), calls=%async_computation.11 | async-start | bytes 2424832 | tf_op jit(solution)/shard_map/all_to_all | solution.py:19
  402.4 3.4 copy-start.3
  431.0 59.4 %all-to-all-start.4 = ((f32[4,32,4736]{2,1,0:T(8,128)}), f32[4,32,4736]{2,1,0:T(8,128)}, u32[]{:S(2)}, u32[]{:S(2)}) async-start(f32[4,32,4736]{2,1,0:T(8,128)} %bitcast.81), calls=%async_computation.7 | async-start | bytes 4849664 | tf_op jit(solution)/shard_map/all_to_all | solution.py:19
  490.4 59.5 %all-to-all-start.5 = ((f32[4,32,4736]{2,1,0:T(8,128)}), f32[4,32,4736]{2,1,0:T(8,128)}, u32[]{:S(2)}, u32[]{:S(2)}) async-start(f32[4,32,4736]{2,1,0:T(8,128)} %bitcast.80), calls=%async_computation.8 | async-start | bytes 4849664 | tf_op jit(solution)/shard_map/all_to_all | solution.py:19
  554.7 58.4 %all-to-all-start.6 = ((f32[4,32,4736]{2,1,0:T(8,128)}), f32[4,32,4736]{2,1,0:T(8,128)S(1)}, u32[]{:S(2)}, u32[]{:S(2)}) async-start(f32[4,32,4736]{2,1,0:T(8,128)} %bitcast.90), calls=%async_computation.9 | async-start | bytes 4849664 | tf_op jit(solution)/shard_map/all_to_all | solution.py:19
  561.2 3.4 copy-start.4
  613.1 2.0 copy-start.1
  613.3 3.0 copy-start
  624.3 2.6 copy-start.5
  626.8 1.8 copy-start.6
  626.8 2.5 copy-start.7
Sparse Core Ops, SparseCore 0:
  36.8 131.5 reduce-scatter.6
  171.9 78.0 reduce-scatter.10
  253.7 128.8 reduce-scatter.4
  386.0 128.8 reduce-scatter.8
